TPU v7x, 32 devices: a whole 2x2x4 slice. The times are simulated.
32 devices in a mesh: blk: 16 (over z, y, x), grp: 2 (over core).
Axes of the slice: x: 2, y: 2, z: 4, core: 2. Of those that a mesh axis runs over, the one named last changes fastest.
Arguments:
- sky_maps: float32 [4, 128, 4096], P(None, ('blk', 'grp')), may hold values from -6 to 6
- legendre: bfloat16 [128, 512, 2048], P(('blk', 'grp')), may hold values from -0.5 to 0.5
- owner_table: int32 [512], replicated, may hold values from 0 to 511, each once
Outputs:
- harmonics: float32 [512, 4, 2, 2048], P(('blk', 'grp'))
- spectra: float32 [10, 2048], P(None, ('blk', 'grp'))
Inputs may be any that keep to these rules, and one draw needn't show every extreme that they name: `owner_table`: a permutation of the orders 0 to 511.
All inputs are finite; a program needn't handle non-finite values.
Results may differ from a plain program's by a relative error of at most 0.0034.
Values may be sent and summed in bfloat16 or wider, within the bound.
A program may use at most 128 MiB of HBM per device.

v0:
```python
import math
import jax
import jax.numpy as jnp
import numpy as np
from jax import lax
from jax.sharding import PartitionSpec as P


def cycle_fourier(sky_maps, order_count):
    map_count, cycle_count, pixels = sky_maps.shape
    pixel_index = lax.iota(jnp.int32, pixels)
    order_index = lax.iota(jnp.int32, order_count)
    phase = (pixel_index[:, None] * order_index[None, :] % pixels).astype(jnp.float32) * (
        2.0 * math.pi / pixels
    )
    table = jnp.concatenate([jnp.cos(phase), -jnp.sin(phase)], axis=1) / math.sqrt(pixels)
    flat = sky_maps.reshape(map_count * cycle_count, pixels)
    spectral = jnp.dot(
        flat, table, precision=lax.Precision.HIGHEST, preferred_element_type=jnp.float32
    )
    spectral = spectral.reshape(map_count, cycle_count, 2, order_count)
    spectral = jnp.transpose(spectral, (1, 0, 2, 3)).reshape(
        cycle_count, 2 * map_count, order_count
    )
    return spectral.astype(jnp.bfloat16)


def per_device(sky_maps, legendre, owner_table):
    map_count = sky_maps.shape[0]
    order_count = legendre.shape[1]
    ell_count = legendre.shape[2]
    devices_all = lax.axis_size(("blk", "grp"))
    own_count = order_count // devices_all
    my_index = lax.axis_index(("blk", "grp"))
    owned_orders = lax.dynamic_slice_in_dim(owner_table, my_index * own_count, own_count)
    fourier = cycle_fourier(sky_maps, order_count)
    table_perm = jnp.take(legendre, owner_table, axis=1)
    fourier_perm = jnp.take(fourier, owner_table, axis=2)
    four_cols = jnp.transpose(fourier_perm, (0, 2, 1))
    table_own, four_own = (
        lax.all_to_all(table_perm, ("blk", "grp"), split_axis=1, concat_axis=0, tiled=True),
        lax.all_to_all(four_cols, ("blk", "grp"), split_axis=1, concat_axis=0, tiled=True),
    )
    summed = jnp.einsum("rmc,rml->mcl", four_own, table_own, preferred_element_type=jnp.float32)
    ell_index = lax.iota(jnp.int32, ell_count)
    keep = ell_index[None, None, :] >= owned_orders[:, None, None]
    summed = jnp.where(keep, summed, jnp.zeros_like(summed))
    harmonics = summed.reshape(own_count, map_count, 2, ell_count)
    weight = jnp.where(owned_orders == 0, 1.0, 2.0).astype(jnp.float32)
    cross = jnp.einsum("m,miql,mjql->ijl", weight, harmonics, harmonics)
    first_map, second_map = np.triu_indices(map_count)
    pair_terms = cross[first_map, second_map]
    ell_share = ell_count // devices_all
    owned_power = lax.psum_scatter(pair_terms, ("blk", "grp"), scatter_dimension=1, tiled=True)
    owned_ells = my_index * ell_share + lax.iota(jnp.int32, ell_share)
    spectra = owned_power / (2 * owned_ells + 1).astype(jnp.float32)[None, :]
    return (harmonics, spectra)


def solution(mesh):
    return jax.shard_map(
        per_device,
        mesh=mesh,
        in_specs=(P(None, ("blk", "grp"), None), P(("blk", "grp"), None, None), P()),
        out_specs=(P(("blk", "grp"), None, None, None), P(None, ("blk", "grp"))),
        check_vma=False,
    )
```

profile of v0, /device:TPU:0, one launch (start us, length us, event | category | flops | bytes accessed | tf_op | source)
XLA Modules:
  0.0 506.8 jit_solution(16573717867274145722)
XLA Ops:
  7.2 34.6 %sine_negate_fusion = (f32[4096,512]{1,0:T(8,128)}, f32[4096,512]{1,0:T(8,128)}) fusion(), kind=kLoop, calls=%fused_computation.16 | loop fusion | flops 31457280 | bytes 16777216 | tf_op jit(solution)/shard_map/neg | solution.py:16
  41.9 0.1 reshape.47
  42.0 12.7 %fusion.12 = bf16[16,1024]{1,0:T(8,128)(2,1)S(1)} fusion(f32[16,4096]{1,0:T(8,128)S(1)} %reshape.47, f32[4096,512]{1,0:T(8,128)} %get-tuple-element.4, f32[4096,512]{1,0:T(8,128)} %get-tuple-element.5), kind=kOutput, calls=%fused_computation.24 | convolution fusion | flops 813711360 | bytes 17072128 | tf_op jit(solution)/shard_map/dot_general | solution.py:18
  54.7 0.3 copy.23
  55.0 2.1 gather_fusion
  57.1 1.8 fusion.15
  58.9 1.2 reshape.76
  60.0 7.3 %all-to-all-start = ((bf16[32,2,256]{2,1,0:T(2,128)(2,1)}), bf16[32,2,256]{2,1,0:T(2,128)(2,1)S(1)}, u32[]{:S(2)}, u32[]{:S(2)}) async-start(bf16[32,2,256]{2,1,0:T(2,128)(2,1)} %reshape.76), calls=%async_computation | async-start | bytes 65536 | tf_op jit(solution)/shard_map/all_to_all | solution.py:42
  67.4 35.2 %gather_fusion.1 = bf16[512,4,2048]{2,0,1:T(8,128)(2,1)} fusion(bf16[4,512,2048]{2,1,0:T(8,128)(2,1)} %param.8, s32[1024]{0:T(1024)S(1)} %pad_clamp_fusion), kind=kCustom, calls=%fused_computation.1 | custom fusion | bytes 16779264 | tf_op jit(solution)/shard_map/jit(_take)/gather | solution.py:37
  102.5 7.6 %select_bitcast_fusion = bf16[4,512,2048]{2,1,0:T(8,128)(2,1)} fusion(bf16[512,4,2048]{2,0,1:T(8,128)(2,1)} %gather_fusion.1, pred[512]{0:T(512)(128)(4,1)S(1)} %compare_and_fusion), kind=kLoop, calls=%fused_computation.14 | loop fusion | flops 4194304 | bytes 16777728 | tf_op jit(solution)/shard_map/jit(_take)/select_n | solution.py:37
  110.1 12.1 %copy.26 = bf16[4,512,2048]{2,0,1:T(4,128)(2,1)} copy(bf16[4,512,2048]{2,1,0:T(8,128)(2,1)} %select_bitcast_fusion) | data formatting | bytes 16777216 | tf_op jit(solution)/shard_map/jit(_take)/select_n | solution.py:37
  122.2 6.0 %all-to-all-start.1 = ((bf16[4,512,2048]{2,0,1:T(4,128)(2,1)}), bf16[4,512,2048]{2,0,1:T(4,128)(2,1)}, u32[]{:S(2)}, u32[]{:S(2)}) async-start(bf16[4,512,2048]{2,0,1:T(4,128)(2,1)} %copy.26), calls=%async_computation.1 | async-start | bytes 16777216 | tf_op jit(solution)/shard_map/all_to_all | solution.py:41
  128.3 0.1 compare_select_fusion.1
  128.3 0.1 iota_compare_fusion
  128.4 0.6 reshape.77
  129.1 0.3 copy.34
  129.4 0.2 copy.28
  129.6 184.5 %all-to-all-done.1 = bf16[4,512,2048]{2,0,1:T(4,128)(2,1)} async-done(((bf16[4,512,2048]{2,0,1:T(4,128)(2,1)}), bf16[4,512,2048]{2,0,1:T(4,128)(2,1)}, u32[]{:S(2)}, u32[]{:S(2)}) %all-to-all-start.1) | async-done | bytes 8388640 | tf_op jit(solution)/shard_map/all_to_all | solution.py:41
  314.1 8.5 %copy.38 = bf16[4,32,16,2048]{3,0,1,2:T(4,128)(2,1)} copy(bf16[4,32,16,2048]{3,0,2,1:T(4,128)(2,1)} %bitcast.9) | data formatting | bytes 16777216 | tf_op jit(solution)/shard_map/all_to_all | solution.py:41
  322.6 12.6 %all_to_all.33 = bf16[128,16,2048]{2,0,1:T(8,128)(2,1)} reshape(bf16[32,4,16,2048]{3,1,0,2:T(4,128)(2,1)} %bitcast.37) | data formatting | bytes 16777216 | tf_op jit(solution)/shard_map/all_to_all | solution.py:41
  335.2 4.6 convolution_select_fusion
  339.8 0.6 reshape.48
  340.4 5.5 %copy.30 = bf16[16,4,2,2048]{0,1,2,3:T(4,128)(2,1)} copy(f32[16,4,2,2048]{3,2,1,0:T(2,128)S(1)} %reshape.48) | data formatting | bytes 1572864 | tf_op jit(solution)/shard_map/reshape | solution.py:48
  345.9 0.5 broadcast_multiply_fusion
  346.4 4.9 copy.29
  351.3 7.8 %convolution_bitcast_fusion = f32[4,4,2048]{1,0,2:T(4,128)} fusion(bf16[16,4,2,2048]{0,1,2,3:T(4,128)(2,1)} %copy.29, bf16[16,4,2,2048]{0,1,2,3:T(4,128)(2,1)} %copy.30), kind=kOutput, calls=%fused_computation.22 | convolution fusion | flops 2097152 | bytes 1179648 | tf_op jit(solution)/shard_map/m,miql,mjql->ijl/dot_general | solution.py:50
  359.1 3.6 copy.31
  362.6 0.8 gather_fusion.2
  363.4 1.3 copy.35
  364.8 133.7 %reduce-scatter.4.cloned.1.call-done = f32[64,10]{1,0:T(8,128)} async-done(((f32[2048,10]{1,0:T(8,128)}), f32[64,10]{1,0:T(8,128)}) %reduce-scatter.4.cloned.1.call-update) | async-done | bytes 2576
  498.5 0.8 copy.36
  499.4 0.6 broadcast_divide_fusion
  (17 shorter events, 0.1 us)
Async XLA Ops:
  7.2 34.6 %copy-start.3 = (s32[512]{0:T(512)S(1)}, s32[512]{0:T(512)}, u32[]{:S(2)}) copy-start(s32[512]{0:T(512)} %param.9) | copy-start | bytes 6148
  7.2 34.7 %copy-start.1 = (f32[4,4,4096]{2,1,0:T(4,128)S(1)}, f32[4,4,4096]{2,1,0:T(4,128)}, u32[]{:S(2)}) copy-start(f32[4,4,4096]{2,1,0:T(4,128)} %param.7) | copy-start | bytes 786436
  60.0 62.2 %all-to-all-start = ((bf16[32,2,256]{2,1,0:T(2,128)(2,1)}), bf16[32,2,256]{2,1,0:T(2,128)(2,1)S(1)}, u32[]{:S(2)}, u32[]{:S(2)}) async-start(bf16[32,2,256]{2,1,0:T(2,128)(2,1)} %reshape.76), calls=%async_computation | async-start | bytes 65536 | tf_op jit(solution)/shard_map/all_to_all | solution.py:42
  122.2 191.9 %all-to-all-start.1 = ((bf16[4,512,2048]{2,0,1:T(4,128)(2,1)}), bf16[4,512,2048]{2,0,1:T(4,128)(2,1)}, u32[]{:S(2)}, u32[]{:S(2)}) async-start(bf16[4,512,2048]{2,0,1:T(4,128)(2,1)} %copy.26), calls=%async_computation.1 | async-start | bytes 16777216 | tf_op jit(solution)/shard_map/all_to_all | solution.py:41
  128.2 370.3 %reduce-scatter.4.cloned.1.call-start = ((), (), s32[]{:S(2)}) async-start(), calls=%async_computation.3 | async-start | bytes 1081344
  340.4 18.7 %copy-start = (f32[16,4,2,2048]{3,2,1,0:T(2,128)}, f32[16,4,2,2048]{3,2,1,0:T(2,128)S(1)}, u32[]{:S(2)}) copy-start(f32[16,4,2,2048]{3,2,1,0:T(2,128)S(1)} %reshape.48) | copy-start | bytes 3145732
  351.3 11.3 %copy-start.2 = (s32[10]{0:T(128)S(1)}, s32[10]{0:T(128)}, u32[]{:S(2)}) copy-start(s32[10]{0:T(128)} %constant.109) | copy-start | bytes 124
Sparse Core Ops, SparseCore 0:
  364.9 133.5 reduce-scatter.3
where the time goes:
time: 508 us; the launch traced here: 507 us
  waiting for transfers between devices  318 us (63%)
  local copies, waits for them, and re-layouts  90.7 us (18%)
  other arithmetic  45.3 us (9%)
  matrix products  25 us (5%)
  between operations  14.2 us (3%)
  starting transfers between devices  13.3 us (3%)
    all_to_all x1, waiting for transfers between devices, per_device(): lax.all_to_all(table_perm, ('blk', 'grp'), split_axis=1, concat_axis=0, t...  185 us
    unnamed x2, waiting for transfers between devices  134 us
    gather x1, local copies, waits for them, and re-layouts, per_device(): table_perm = jnp.take(legendre, owner_table, axis=1)  35.2 us
    neg x1, other arithmetic, cycle_fourier(): -jnp.sin(phase)  34.6 us
    all_to_all x2, local copies, waits for them, and re-layouts, per_device(): lax.all_to_all(table_perm, ('blk', 'grp'), split_axis=1, concat_axis=0, t...  21.1 us
    dot_general x1, matrix products, cycle_fourier(): jnp.dot(flat, table, precision=lax.Precision.HIGHEST, preferred_element_t...  12.7 us
    select_n x1, local copies, waits for them, and re-layouts, per_device(): table_perm = jnp.take(legendre, owner_table, axis=1)  12.1 us
  transfers between devices with their start and end apart: 3, of which 2 were waited for; matrix products, arithmetic and copies ran while one was open for 11% of the time, Pallas kernels for 0%

commit v1 on v0

--- a/solution.py
+++ b/solution.py
@@ -4,6 +4,13 @@
 import numpy as np
 from jax import lax
 from jax.sharding import PartitionSpec as P
+
+
+def trade_parts(value, axis, split, join):
+    peers = lax.axis_size(axis)
+    blocks = jnp.stack(jnp.split(value, peers, axis=split), axis=0)
+    blocks = lax.all_to_all(blocks, axis, split_axis=0, concat_axis=0)
+    return jnp.concatenate(blocks, axis=join)
 
 
 def cycle_fourier(sky_maps, order_count):
@@ -38,7 +45,7 @@
     fourier_perm = jnp.take(fourier, owner_table, axis=2)
     four_cols = jnp.transpose(fourier_perm, (0, 2, 1))
     table_own, four_own = (
-        lax.all_to_all(table_perm, ("blk", "grp"), split_axis=1, concat_axis=0, tiled=True),
+        trade_parts(table_perm, ("blk", "grp"), 1, 0),
         lax.all_to_all(four_cols, ("blk", "grp"), split_axis=1, concat_axis=0, tiled=True),
     )
     summed = jnp.einsum("rmc,rml->mcl", four_own, table_own, preferred_element_type=jnp.float32)

time: 508 us -> 544 us (1.071); the launches traced: 507 us -> 536 us
  local copies, waits for them, and re-layouts: 90.7 us -> 112 us
  matrix products: 25 us -> 32.7 us
    unnamed x12 -> x43, local copies, waits for them, and re-layouts: 3.99 us -> 56 us
    all_to_all x2 -> x0, local copies, waits for them, and re-layouts: 21.1 us -> none  [per_device(): lax.all_to_all(table_perm, ('blk', 'grp'), split_axis=1, concat_axis=0, t...]
    select_n x1 -> x0, local copies, waits for them, and re-layouts: 12.1 us -> none  [per_device(): table_perm = jnp.take(legendre, owner_table, axis=1)]
    dot_general x1, matrix products: 4.58 us -> 12.3 us  [per_device(): jnp.einsum('rmc,rml->mcl', four_own, table_own, preferred_element_type=jn...]
  transfers between devices with their start and end apart: 3 -> 3, of which waited for: 2 -> 2; matrix products, arithmetic and copies ran while one was open for 11% -> 18% of each run, Pallas kernels for 0% -> 0%
where the time goes in v1:
time: 544 us; the launch traced here: 536 us
  waiting for transfers between devices  318 us (58%)
  local copies, waits for them, and re-layouts  112 us (21%)
  other arithmetic  45.3 us (8%)
  matrix products  32.7 us (6%)
  between operations  14.5 us (3%)
  starting transfers between devices  13.3 us (2%)
    all_to_all x1, waiting for transfers between devices, trade_parts(): blocks = lax.all_to_all(blocks, axis, split_axis=0, concat_axis=0)  185 us
    unnamed x2, waiting for transfers between devices  134 us
    unnamed x43, local copies, waits for them, and re-layouts  56 us
    gather x1, local copies, waits for them, and re-layouts, per_device(): table_perm = jnp.take(legendre, owner_table, axis=1)  35.4 us
    neg x1, other arithmetic, cycle_fourier(): -jnp.sin(phase)  34.6 us
    dot_general x1, matrix products, cycle_fourier(): jnp.dot(flat, table, precision=lax.Precision.HIGHEST, preferred_element_t...  12.7 us
    dot_general x1, matrix products, per_device(): jnp.einsum('rmc,rml->mcl', four_own, table_own, preferred_element_type=jn...  12.3 us
  transfers between devices with their start and end apart: 3, of which 2 were waited for; matrix products, arithmetic and copies ran while one was open for 18% of the time, Pallas kernels for 0%

profile of v1, /device:TPU:0, one launch (start us, length us, event | category | flops | bytes accessed | tf_op | source)
XLA Modules:
  0.0 535.7 jit_solution(10152660609685607328)
XLA Ops:
  7.2 34.6 %sine_negate_fusion = (f32[4096,512]{1,0:T(8,128)}, f32[4096,512]{1,0:T(8,128)}) fusion(), kind=kLoop, calls=%fused_computation.17 | loop fusion | flops 31457280 | bytes 16777216 | tf_op jit(solution)/shard_map/neg | solution.py:23
  42.0 12.7 %fusion.17 = bf16[16,1024]{1,0:T(8,128)(2,1)S(1)} fusion(f32[16,4096]{1,0:T(8,128)S(1)} %reshape.50, f32[4096,512]{1,0:T(8,128)} %get-tuple-element.4, f32[4096,512]{1,0:T(8,128)} %get-tuple-element.5), kind=kOutput, calls=%fused_computation.25 | convolution fusion | flops 813711360 | bytes 17072128 | tf_op jit(solution)/shard_map/dot_general | solution.py:25
  55.0 2.1 gather_fusion
  57.1 1.8 fusion.52
  60.0 7.3 %all-to-all-start = ((bf16[32,2,256]{2,1,0:T(2,128)(2,1)}), bf16[32,2,256]{2,1,0:T(2,128)(2,1)S(1)}, u32[]{:S(2)}, u32[]{:S(2)}) async-start(bf16[32,2,256]{2,1,0:T(2,128)(2,1)} %reshape.80), calls=%async_computation | async-start | bytes 65536 | tf_op jit(solution)/shard_map/all_to_all | solution.py:49
  67.4 35.4 %gather_fusion.1 = bf16[512,4,2048]{2,0,1:T(8,128)(2,1)} fusion(bf16[4,512,2048]{2,1,0:T(8,128)(2,1)} %param.8, s32[1024]{0:T(1024)S(1)} %pad_clamp_fusion), kind=kCustom, calls=%fused_computation.1 | custom fusion | bytes 16779264 | tf_op jit(solution)/shard_map/jit(_take)/gather | solution.py:44
  102.8 7.6 %select_bitcast_fusion = bf16[4,512,2048]{2,1,0:T(8,128)(2,1)} fusion(bf16[512,4,2048]{2,0,1:T(8,128)(2,1)} %gather_fusion.1, pred[512]{0:T(512)(128)(4,1)S(1)} %compare_and_fusion), kind=kLoop, calls=%fused_computation.15 | loop fusion | flops 4194304 | bytes 16777728 | tf_op jit(solution)/shard_map/jit(_take)/select_n | solution.py:44
  110.3 1.7 fusion.49
  112.1 1.7 fusion.48
  113.7 1.7 fusion.47
  115.4 1.7 fusion.46
  118.8 1.7 fusion.44
  122.1 1.7 fusion.42
  123.8 1.7 fusion.41
  127.1 1.7 fusion.39
  130.5 1.7 fusion.37
  135.5 1.7 fusion.34
  138.8 1.7 fusion.32
  140.5 1.7 fusion.31
  145.5 1.7 fusion.28
  150.6 1.7 fusion.25
  153.9 1.7 fusion.23
  157.3 1.7 fusion.21
  159.0 1.7 fusion.20
  164.0 6.0 %all-to-all-start.1 = ((bf16[32,4,16,2048]{3,2,1,0:T(8,128)(2,1)}), bf16[32,4,16,2048]{3,2,1,0:T(8,128)(2,1)}, u32[]{:S(2)}, u32[]{:S(2)}) async-start(bf16[32,4,16,2048]{3,2,1,0:T(8,128)(2,1)} %fusion.18), calls=%async_computation.1 | async-start | bytes 16777216 | tf_op jit(solution)/shard_map/all_to_all | solution.py:12
  171.3 184.5 %all-to-all-done.1 = bf16[32,4,16,2048]{3,2,1,0:T(8,128)(2,1)} async-done(((bf16[32,4,16,2048]{3,2,1,0:T(8,128)(2,1)}), bf16[32,4,16,2048]{3,2,1,0:T(8,128)(2,1)}, u32[]{:S(2)}, u32[]{:S(2)}) %all-to-all-start.1) | async-done | bytes 8388640 | tf_op jit(solution)/shard_map/all_to_all | solution.py:12
  355.9 12.3 %fusion.13 = f32[16,8,2048]{2,1,0:T(8,128)S(1)} fusion(bf16[128,16,8]{0,2,1:T(8,128)(2,1)S(1)} %copy.27, bf16[128,16,2048]{2,1,0:T(8,128)(2,1)} %bitcast.41, pred[16,2048]{1,0:T(8,128)(4,1)S(1)} %iota_compare_fusion), kind=kOutput, calls=%fused_computation.22 | convolution fusion | flops 67371008 | bytes 9502720 | tf_op jit(solution)/shard_map/rmc,rml->mcl/dot_general | solution.py:51
  368.8 5.7 %copy.29 = bf16[16,4,2,2048]{0,1,2,3:T(4,128)(2,1)} copy(f32[16,4,2,2048]{3,2,1,0:T(2,128)S(1)} %reshape.52) | data formatting | bytes 1572864 | tf_op jit(solution)/shard_map/reshape | solution.py:55
  375.0 4.9 copy.28
  380.0 7.8 %convolution_bitcast_fusion = f32[4,4,2048]{1,0,2:T(4,128)} fusion(bf16[16,4,2,2048]{0,1,2,3:T(4,128)(2,1)} %copy.28, bf16[16,4,2,2048]{0,1,2,3:T(4,128)(2,1)} %copy.29), kind=kOutput, calls=%fused_computation.23 | convolution fusion | flops 2097152 | bytes 1179648 | tf_op jit(solution)/shard_map/m,miql,mjql->ijl/dot_general | solution.py:57
  387.7 3.6 copy.30
  393.4 133.7 %reduce-scatter.4.cloned.1.call-done = f32[64,10]{1,0:T(8,128)} async-done(((f32[2048,10]{1,0:T(8,128)}), f32[64,10]{1,0:T(8,128)}) %reduce-scatter.4.cloned.1.call-update) | async-done | bytes 2576
  (46 shorter events, 32.7 us)
Async XLA Ops:
  7.2 34.6 %copy-start.3 = (s32[512]{0:T(512)S(1)}, s32[512]{0:T(512)}, u32[]{:S(2)}) copy-start(s32[512]{0:T(512)} %param.9) | copy-start | bytes 6148
  7.2 34.7 %copy-start.1 = (f32[4,4,4096]{2,1,0:T(4,128)S(1)}, f32[4,4,4096]{2,1,0:T(4,128)}, u32[]{:S(2)}) copy-start(f32[4,4,4096]{2,1,0:T(4,128)} %param.7) | copy-start | bytes 786436
  60.0 104.0 %all-to-all-start = ((bf16[32,2,256]{2,1,0:T(2,128)(2,1)}), bf16[32,2,256]{2,1,0:T(2,128)(2,1)S(1)}, u32[]{:S(2)}, u32[]{:S(2)}) async-start(bf16[32,2,256]{2,1,0:T(2,128)(2,1)} %reshape.80), calls=%async_computation | async-start | bytes 65536 | tf_op jit(solution)/shard_map/all_to_all | solution.py:49
  164.0 191.9 %all-to-all-start.1 = ((bf16[32,4,16,2048]{3,2,1,0:T(8,128)(2,1)}), bf16[32,4,16,2048]{3,2,1,0:T(8,128)(2,1)}, u32[]{:S(2)}, u32[]{:S(2)}) async-start(bf16[32,4,16,2048]{3,2,1,0:T(8,128)(2,1)} %fusion.18), calls=%async_computation.1 | async-start | bytes 16777216 | tf_op jit(solution)/shard_map/all_to_all | solution.py:12
  170.0 357.2 %reduce-scatter.4.cloned.1.call-start = ((), (), s32[]{:S(2)}) async-start(), calls=%async_computation.3 | async-start | bytes 1081344
  368.8 18.9 %copy-start = (f32[16,4,2,2048]{3,2,1,0:T(2,128)}, f32[16,4,2,2048]{3,2,1,0:T(2,128)S(1)}, u32[]{:S(2)}) copy-start(f32[16,4,2,2048]{3,2,1,0:T(2,128)S(1)} %reshape.52) | copy-start | bytes 3145732
  380.0 11.3 %copy-start.2 = (s32[10]{0:T(128)S(1)}, s32[10]{0:T(128)}, u32[]{:S(2)}) copy-start(s32[10]{0:T(128)} %constant.109) | copy-start | bytes 124
Sparse Core Ops, SparseCore 0:
  393.5 133.5 reduce-scatter.3
